TPU v7x, 32 devices: a whole 2x2x4 slice. The times are simulated.
32 devices in a mesh: blk: 32 (over z, y, x, core).
Axes of the slice: x: 2, y: 2, z: 4, core: 2. Of those that a mesh axis runs over, the one named last changes fastest.
Arguments:
- samples: bfloat16 [8192, 2048], P('blk'), may hold values from -6 to 6
- hubs: int32 [64], replicated, may hold values from 0 to 8191, as said below
- start: int32 [1], replicated, may hold values from 1 to 13
Outputs:
- self_stat: float32 [8192, 256], P('blk')
- ahead_stat: float32 [3, 8192, 256], P(None, 'blk')
- behind_stat: float32 [3, 8192, 256], P(None, 'blk')
Inputs may be any that keep to these rules, and one draw needn't show every extreme that they name: `hubs`: the 64 indices are distinct.
All inputs are finite; a program needn't handle non-finite values.
Results may differ from a plain program's by a relative error of at most 0.0049.
Values may be sent and summed in bfloat16 or wider, within the bound.
No kernel may reach another device: no remote copies, remote signals or barrier semaphores. Data moves between devices by JAX's collectives and lax.ppermute only.
A program may use at most 64 MiB of HBM per device.

v0:
```python
import math
import jax
import jax.numpy as jnp
from jax import lax
from jax.sharding import PartitionSpec as P


def shifted(block, axis, distance):
    devices = range(lax.axis_size(axis))
    route = [((i - distance) % len(devices), i) for i in devices]
    return lax.ppermute(block, axis, route)


def row_scale(resid):
    wide = resid.astype(jnp.float32)
    return 1.0 / jnp.sqrt(jnp.maximum(jnp.sum(wide * wide, axis=1), 1.0))


def correlate(resid, scale, partner):
    dots = lax.dot_general(
        resid, partner, (((1,), (1,)), ((), ())), preferred_element_type=jnp.float32
    )
    return (dots * scale[:, None] * row_scale(partner)[None, :]).astype(jnp.bfloat16)


def to_stat(rounded, factor):
    values = lax.optimization_barrier(rounded).astype(jnp.float32)
    return factor * (0.5 * (jnp.log1p(values) - jnp.log1p(-values)))


def shards(samples, hubs, start):
    rows = samples.shape[0]
    width = samples.shape[1]
    factor = math.sqrt(width - hubs.shape[0] - 3)
    count = lax.axis_size("blk")
    mine = lax.axis_index("blk")
    levels = count.bit_length() - 2
    offset = start[0]
    owner = hubs // rows
    within = hubs % rows
    picker = jnp.logical_and(
        (owner == mine)[:, None], within[:, None] == jnp.arange(rows, dtype=jnp.int32)[None, :]
    ).astype(jnp.bfloat16)
    hub_rows = lax.psum(jnp.dot(picker, samples, preferred_element_type=jnp.float32), "blk")
    gram = jnp.dot(hub_rows, hub_rows.T, precision=lax.Precision.HIGHEST)
    proj = jnp.dot(samples, hub_rows.astype(jnp.bfloat16).T, preferred_element_type=jnp.float32)
    factor_lower = jnp.linalg.cholesky(gram)
    coef = jax.scipy.linalg.cho_solve((factor_lower, True), proj.T).T
    resid = (
        samples.astype(jnp.float32) - jnp.dot(coef, hub_rows, precision=lax.Precision.HIGHEST)
    ).astype(jnp.bfloat16)
    scale = row_scale(resid)
    own = correlate(resid, scale, resid)
    diag = jnp.arange(rows)[:, None] == jnp.arange(rows)[None, :]
    own_stat = jnp.where(diag, 0.0, to_stat(own, factor))
    partner = resid
    for level in range(levels):
        moved = shifted(partner, "blk", -(1 << level))
        partner = jnp.where(offset >> level & 1 == 1, moved, partner)
    ahead = []
    turned = []
    for index in range(3):
        if index > 0:
            partner = shifted(partner, "blk", -1)
        tile = correlate(resid, scale, partner)
        ahead.append(to_stat(tile, factor))
        turned.append(tile.T)
    returned = []
    for index in range(3):
        tile = turned[index]
        for extra in range(index):
            tile = shifted(tile, "blk", 1)
        for level in range(levels):
            moved = shifted(tile, "blk", 1 << level)
            tile = jnp.where(offset >> level & 1 == 1, moved, tile)
        returned.append(tile)
    behind = jnp.stack([to_stat(tile, factor) for tile in returned])
    return (own_stat, jnp.stack(ahead), behind)


def solution(mesh):
    in_specs = (P("blk", None), P(), P())
    out_specs = (P("blk", None), P(None, "blk", None), P(None, "blk", None))
    return jax.shard_map(shards, mesh=mesh, in_specs=in_specs, out_specs=out_specs, check_vma=False)
```

profile of v0, /device:TPU:0, one launch (start us, length us, event | category | flops | bytes accessed | tf_op | source)
XLA Modules:
  0.0 362.8 jit_solution(15652582608777804637)
XLA Ops:
  7.2 0.7 and_select_fusion
  7.9 0.7 fusion.50
  8.5 2.4 fusion.40
  10.9 134.7 %all-reduce.2.cloned.1.call-done = f32[64,2048]{1,0:T(8,128)} async-done(((f32[64,2048]{1,0:T(8,128)}), f32[64,2048]{1,0:T(8,128)}) %all-reduce.2.cloned.1.call-update) | async-done | bytes 524304 | tf_op jit(solution)/shard_map/psum | solution.py:44
  145.6 1.8 fusion.51
  147.6 5.8 %cholesky.16 = f32[64,64]{1,0:T(8,128)S(1)} custom-call(f32[64,64]{1,0:T(8,128)S(1)} %fusion.47), custom_call_target="Cholesky" | custom-call | tf_op jit(solution)/shard_map/jit(cholesky)/cholesky | solution.py:47
  153.4 0.6 compare_reduce_fusion
  154.1 0.7 fusion.42
  154.7 4.9 %custom-call.10 = f32[1,64,64]{1,2,0:T(8,128)S(1)} custom-call(f32[1,64,64]{2,1,0:T(8,128)S(1)} %fusion.42), custom_call_target="InvertDiagBlocksLowerTriangular" | custom-call | tf_op jit(solution)/shard_map/jit(_cho_solve)/triangular_solve | solution.py:48
  159.7 0.4 fusion.37
  160.1 0.3 fusion.45
  160.6 2.1 multiply_reduce_fusion.3
  162.6 1.9 collective-permute-start
  165.2 11.7 %collective-permute-done = bf16[256,2048]{1,0:T(8,128)(2,1)S(1)} collective-permute-done((bf16[256,2048]{1,0:T(8,128)(2,1)S(1)}, bf16[256,2048]{1,0:T(8,128)(2,1)S(1)}, u32[]{:S(2)}, u32[]{:S(2)}) %collective-permute-start) | collective-permute-done | bytes 1048608 | tf_op jit(solution)/shard_map/ppermute | solution.py:11
  177.0 1.4 collective-permute-start.1
  178.4 23.6 %collective-permute-done.1 = bf16[256,2048]{1,0:T(8,128)(2,1)S(1)} collective-permute-done((bf16[256,2048]{1,0:T(8,128)(2,1)S(1)}, bf16[256,2048]{1,0:T(8,128)(2,1)S(1)}, u32[]{:S(2)}, u32[]{:S(2)}) %collective-permute-start.1) | collective-permute-done | bytes 1048608 | tf_op jit(solution)/shard_map/ppermute | solution.py:11
  202.1 0.8 collective-permute-start.2
  202.9 24.4 %collective-permute-done.2 = bf16[256,2048]{1,0:T(8,128)(2,1)S(1)} collective-permute-done((bf16[256,2048]{1,0:T(8,128)(2,1)S(1)}, bf16[256,2048]{1,0:T(8,128)(2,1)S(1)}, u32[]{:S(2)}, u32[]{:S(2)}) %collective-permute-start.2) | collective-permute-done | bytes 1048608 | tf_op jit(solution)/shard_map/ppermute | solution.py:11
  227.4 1.5 collective-permute-start.3
  229.0 22.8 %collective-permute-done.3 = bf16[256,2048]{1,0:T(8,128)(2,1)S(1)} collective-permute-done((bf16[256,2048]{1,0:T(8,128)(2,1)S(1)}, bf16[256,2048]{1,0:T(8,128)(2,1)S(1)}, u32[]{:S(2)}, u32[]{:S(2)}) %collective-permute-start.3) | collective-permute-done | bytes 1048608 | tf_op jit(solution)/shard_map/ppermute | solution.py:11
  251.8 0.5 multiply_reduce_fusion.2
  252.3 6.7 %collective-permute-start.4 = (bf16[256,2048]{1,0:T(8,128)(2,1)S(1)}, bf16[256,2048]{1,0:T(8,128)(2,1)S(1)}, u32[]{:S(2)}, u32[]{:S(2)}) collective-permute-start(bf16[256,2048]{1,0:T(8,128)(2,1)S(1)} %get-tuple-element.7), channel_id=1, source_target_pairs={{1,0},{2,1},{3,2},{4,3},{5,4},{6,5},{7,6},{8,7},{9,8},{10,9},{11,1... | collective-permute-start | bytes 3145736 | tf_op jit(solution)/shard_map/ppermute | solution.py:11
  259.0 0.5 fusion.6
  259.5 0.5 fusion.5
  260.0 7.6 %collective-permute-done.6 = bf16[256,256]{1,0:T(8,128)(2,1)S(1)} collective-permute-done((bf16[256,256]{1,0:T(8,128)(2,1)S(1)}, bf16[256,256]{1,0:T(8,128)(2,1)S(1)}, u32[]{:S(2)}, u32[]{:S(2)}) %collective-permute-start.6) | collective-permute-done | bytes 131104 | tf_op jit(solution)/shard_map/ppermute | solution.py:11
  267.7 0.9 fusion.11
  268.6 7.6 %collective-permute-done.7 = bf16[256,256]{1,0:T(8,128)(2,1)S(1)} collective-permute-done((bf16[256,256]{1,0:T(8,128)(2,1)S(1)}, bf16[256,256]{1,0:T(8,128)(2,1)S(1)}, u32[]{:S(2)}, u32[]{:S(2)}) %collective-permute-start.7) | collective-permute-done | bytes 131104 | tf_op jit(solution)/shard_map/ppermute | solution.py:11
  276.3 0.3 multiply_reduce_fusion.1
  276.6 0.6 fusion.7
  277.3 5.3 %collective-permute-start.5 = (bf16[256,2048]{1,0:T(8,128)(2,1)S(1)}, bf16[256,2048]{1,0:T(8,128)(2,1)S(1)}, u32[]{:S(2)}, u32[]{:S(2)}) collective-permute-start(bf16[256,2048]{1,0:T(8,128)(2,1)S(1)} %collective-permute-done.4), channel_id=1, source_target_pairs={{1,0},{2,1},{3,2},{4,3},{5,4},{6,5},{7,6},{8,7},{9,8},{10,9},{11,1... | collective-permute-start | bytes 3145736 | tf_op jit(solution)/shard_map/ppermute | solution.py:11
  282.8 2.6 collective-permute-done.10
  285.5 8.0 %collective-permute-done.11 = bf16[256,256]{1,0:T(8,128)(2,1)S(1)} collective-permute-done((bf16[256,256]{1,0:T(8,128)(2,1)S(1)}, bf16[256,256]{1,0:T(8,128)(2,1)S(1)}, u32[]{:S(2)}, u32[]{:S(2)}) %collective-permute-start.11) | collective-permute-done | bytes 131104 | tf_op jit(solution)/shard_map/ppermute | solution.py:11
  293.5 4.7 %collective-permute-done.9 = bf16[256,256]{1,0:T(8,128)(2,1)S(1)} collective-permute-done((bf16[256,256]{1,0:T(8,128)(2,1)S(1)}, bf16[256,256]{1,0:T(8,128)(2,1)S(1)}, u32[]{:S(2)}, u32[]{:S(2)}) %collective-permute-start.9) | collective-permute-done | bytes 131104 | tf_op jit(solution)/shard_map/ppermute | solution.py:11
  298.3 5.6 %collective-permute-done.12 = bf16[256,256]{1,0:T(8,128)(2,1)S(1)} collective-permute-done((bf16[256,256]{1,0:T(8,128)(2,1)S(1)}, bf16[256,256]{1,0:T(8,128)(2,1)S(1)}, u32[]{:S(2)}, u32[]{:S(2)}) %collective-permute-start.12) | collective-permute-done | bytes 131104 | tf_op jit(solution)/shard_map/ppermute | solution.py:11
  304.0 0.3 multiply_reduce_fusion
  304.2 0.6 fusion.8
  304.9 6.8 %collective-permute-done.13 = bf16[256,256]{1,0:T(8,128)(2,1)S(1)} collective-permute-done((bf16[256,256]{1,0:T(8,128)(2,1)S(1)}, bf16[256,256]{1,0:T(8,128)(2,1)S(1)}, u32[]{:S(2)}, u32[]{:S(2)}) %collective-permute-start.13) | collective-permute-done | bytes 131104 | tf_op jit(solution)/shard_map/ppermute | solution.py:11
  311.7 2.5 collective-permute-done.15
  314.4 7.8 %collective-permute-done.16 = bf16[256,256]{1,0:T(8,128)(2,1)S(1)} collective-permute-done((bf16[256,256]{1,0:T(8,128)(2,1)S(1)}, bf16[256,256]{1,0:T(8,128)(2,1)S(1)}, u32[]{:S(2)}, u32[]{:S(2)}) %collective-permute-start.16) | collective-permute-done | bytes 131104 | tf_op jit(solution)/shard_map/ppermute | solution.py:11
  322.3 8.0 %collective-permute-done.17 = bf16[256,256]{1,0:T(8,128)(2,1)S(1)} collective-permute-done((bf16[256,256]{1,0:T(8,128)(2,1)S(1)}, bf16[256,256]{1,0:T(8,128)(2,1)S(1)}, u32[]{:S(2)}, u32[]{:S(2)}) %collective-permute-start.17) | collective-permute-done | bytes 131104 | tf_op jit(solution)/shard_map/ppermute | solution.py:11
  330.3 0.4 fusion.27
  330.7 9.5 %collective-permute-done.18 = bf16[256,256]{1,0:T(8,128)(2,1)S(1)} collective-permute-done((bf16[256,256]{1,0:T(8,128)(2,1)S(1)}, bf16[256,256]{1,0:T(8,128)(2,1)S(1)}, u32[]{:S(2)}, u32[]{:S(2)}) %collective-permute-start.18) | collective-permute-done | bytes 131104 | tf_op jit(solution)/shard_map/ppermute | solution.py:11
  340.3 0.2 fusion.23
  340.5 7.5 %collective-permute-done.19 = bf16[256,256]{1,0:T(8,128)(2,1)S(1)} collective-permute-done((bf16[256,256]{1,0:T(8,128)(2,1)S(1)}, bf16[256,256]{1,0:T(8,128)(2,1)S(1)}, u32[]{:S(2)}, u32[]{:S(2)}) %collective-permute-start.19) | collective-permute-done | bytes 131104 | tf_op jit(solution)/shard_map/ppermute | solution.py:11
  348.1 1.1 copy.14
  349.3 5.5 %collective-permute-done.20 = bf16[256,256]{1,0:T(8,128)(2,1)S(1)} collective-permute-done((bf16[256,256]{1,0:T(8,128)(2,1)S(1)}, bf16[256,256]{1,0:T(8,128)(2,1)S(1)}, u32[]{:S(2)}, u32[]{:S(2)}) %collective-permute-start.20) | collective-permute-done | bytes 131104 | tf_op jit(solution)/shard_map/ppermute | solution.py:11
  354.8 0.2 fusion.35
  355.0 0.9 pad_maximum_fusion.1
  (51 shorter events, 2.1 us)
Async XLA Ops:
  7.2 138.5 %all-reduce.2.cloned.1.call-start = ((), (), s32[]{:S(2)}) async-start(), calls=%async_computation | async-start | bytes 1048576 | tf_op jit(solution)/shard_map/psum | solution.py:44
  10.9 148.7 %copy-start = (bf16[256,2048]{1,0:T(8,128)(2,1)S(1)}, bf16[256,2048]{1,0:T(8,128)(2,1)}, u32[]{:S(2)}) copy-start(bf16[256,2048]{1,0:T(8,128)(2,1)} %param.3) | copy-start | bytes 3145732
  145.6 14.0 %copy-start.1 = (f32[64,2048]{1,0:T(8,128)S(1)}, f32[64,2048]{1,0:T(8,128)}, u32[]{:S(2)}) copy-start(f32[64,2048]{1,0:T(8,128)} %all-reduce.2.cloned.1.call-done) | copy-start | bytes 1572868
  162.6 14.2 %collective-permute-start = (bf16[256,2048]{1,0:T(8,128)(2,1)S(1)}, bf16[256,2048]{1,0:T(8,128)(2,1)S(1)}, u32[]{:S(2)}, u32[]{:S(2)}) collective-permute-start(bf16[256,2048]{1,0:T(8,128)(2,1)S(1)} %get-tuple-element.9), channel_id=1, source_target_pairs={{1,0},{2,1},{3,2},{4,3},{5,4},{6,5},{7,6},{8,7},{9,8},{10,9},{11,1... | collective-permute-start | bytes 3145736 | tf_op jit(solution)/shard_map/ppermute | solution.py:11
  177.0 25.0 %collective-permute-start.1 = (bf16[256,2048]{1,0:T(8,128)(2,1)S(1)}, bf16[256,2048]{1,0:T(8,128)(2,1)S(1)}, u32[]{:S(2)}, u32[]{:S(2)}) collective-permute-start(bf16[256,2048]{1,0:T(8,128)(2,1)S(1)} %broadcast_select_fusion), channel_id=1, source_target_pairs={{2,0},{3,1},{4,2},{5,3},{6,4},{7,5},{8,6},{9,7},{10,8},{11,9},{12,... | collective-permute-start | bytes 3145736 | tf_op jit(solution)/shard_map/ppermute | solution.py:11
  202.1 25.2 %collective-permute-start.2 = (bf16[256,2048]{1,0:T(8,128)(2,1)S(1)}, bf16[256,2048]{1,0:T(8,128)(2,1)S(1)}, u32[]{:S(2)}, u32[]{:S(2)}) collective-permute-start(bf16[256,2048]{1,0:T(8,128)(2,1)S(1)} %broadcast_select_fusion.1), channel_id=1, source_target_pairs={{4,0},{5,1},{6,2},{7,3},{8,4},{9,5},{10,6},{11,7},{12,8},{13,9},{1... | collective-permute-start | bytes 3145736 | tf_op jit(solution)/shard_map/ppermute | solution.py:11
  227.4 24.4 %collective-permute-start.3 = (bf16[256,2048]{1,0:T(8,128)(2,1)S(1)}, bf16[256,2048]{1,0:T(8,128)(2,1)S(1)}, u32[]{:S(2)}, u32[]{:S(2)}) collective-permute-start(bf16[256,2048]{1,0:T(8,128)(2,1)S(1)} %broadcast_select_fusion.2), channel_id=1, source_target_pairs={{8,0},{9,1},{10,2},{11,3},{12,4},{13,5},{14,6},{15,7},{16,8},{17,9... | collective-permute-start | bytes 3145736 | tf_op jit(solution)/shard_map/ppermute | solution.py:11
  252.3 24.0 %collective-permute-start.4 = (bf16[256,2048]{1,0:T(8,128)(2,1)S(1)}, bf16[256,2048]{1,0:T(8,128)(2,1)S(1)}, u32[]{:S(2)}, u32[]{:S(2)}) collective-permute-start(bf16[256,2048]{1,0:T(8,128)(2,1)S(1)} %get-tuple-element.7), channel_id=1, source_target_pairs={{1,0},{2,1},{3,2},{4,3},{5,4},{6,5},{7,6},{8,7},{9,8},{10,9},{11,1... | collective-permute-start | bytes 3145736 | tf_op jit(solution)/shard_map/ppermute | solution.py:11
  259.4 8.1 %collective-permute-start.6 = (bf16[256,256]{1,0:T(8,128)(2,1)S(1)}, bf16[256,256]{1,0:T(8,128)(2,1)S(1)}, u32[]{:S(2)}, u32[]{:S(2)}) collective-permute-start(bf16[256,256]{1,0:T(8,128)(2,1)S(1)} %bitcast.47), channel_id=1, source_target_pairs={{31,0},{0,1},{1,2},{2,3},{3,4},{4,5},{5,6},{6,7},{7,8},{8,9},{9,10... | collective-permute-start | bytes 393224 | tf_op jit(solution)/shard_map/ppermute | solution.py:11
  267.6 8.6 %collective-permute-start.7 = (bf16[256,256]{1,0:T(8,128)(2,1)S(1)}, bf16[256,256]{1,0:T(8,128)(2,1)S(1)}, u32[]{:S(2)}, u32[]{:S(2)}) collective-permute-start(bf16[256,256]{1,0:T(8,128)(2,1)S(1)} %broadcast_select_fusion.6), channel_id=1, source_target_pairs={{30,0},{31,1},{0,2},{1,3},{2,4},{3,5},{4,6},{5,7},{6,8},{7,9},{8,1... | collective-permute-start | bytes 393224 | tf_op jit(solution)/shard_map/ppermute | solution.py:11
  276.3 9.1 %collective-permute-start.8 = (bf16[256,256]{1,0:T(8,128)(2,1)S(1)}, bf16[256,256]{1,0:T(8,128)(2,1)S(1)}, u32[]{:S(2)}, u32[]{:S(2)}) collective-permute-start(bf16[256,256]{1,0:T(8,128)(2,1)S(1)} %broadcast_select_fusion.9), channel_id=1, source_target_pairs={{28,0},{29,1},{30,2},{31,3},{0,4},{1,5},{2,6},{3,7},{4,8},{5,9},{6... | collective-permute-start | bytes 393224 | tf_op jit(solution)/shard_map/ppermute | solution.py:11
  277.2 8.2 %collective-permute-start.10 = (bf16[256,256]{1,0:T(8,128)(2,1)S(1)}, bf16[256,256]{1,0:T(8,128)(2,1)S(1)}, u32[]{:S(2)}, u32[]{:S(2)}) collective-permute-start(bf16[256,256]{1,0:T(8,128)(2,1)S(1)} %bitcast.48), channel_id=1, source_target_pairs={{31,0},{0,1},{1,2},{2,3},{3,4},{4,5},{5,6},{6,7},{7,8},{8,9},{9,10... | collective-permute-start | bytes 393224 | tf_op jit(solution)/shard_map/ppermute | solution.py:11
  277.3 26.7 %collective-permute-start.5 = (bf16[256,2048]{1,0:T(8,128)(2,1)S(1)}, bf16[256,2048]{1,0:T(8,128)(2,1)S(1)}, u32[]{:S(2)}, u32[]{:S(2)}) collective-permute-start(bf16[256,2048]{1,0:T(8,128)(2,1)S(1)} %collective-permute-done.4), channel_id=1, source_target_pairs={{1,0},{2,1},{3,2},{4,3},{5,4},{6,5},{7,6},{8,7},{9,8},{10,9},{11,1... | collective-permute-start | bytes 3145736 | tf_op jit(solution)/shard_map/ppermute | solution.py:11
  285.4 8.1 %collective-permute-start.11 = (bf16[256,256]{1,0:T(8,128)(2,1)S(1)}, bf16[256,256]{1,0:T(8,128)(2,1)S(1)}, u32[]{:S(2)}, u32[]{:S(2)}) collective-permute-start(bf16[256,256]{1,0:T(8,128)(2,1)S(1)} %collective-permute-done.10), channel_id=1, source_target_pairs={{31,0},{0,1},{1,2},{2,3},{3,4},{4,5},{5,6},{6,7},{7,8},{8,9},{9,10... | collective-permute-start | bytes 393224 | tf_op jit(solution)/shard_map/ppermute | solution.py:11
  285.4 12.9 %collective-permute-start.9 = (bf16[256,256]{1,0:T(8,128)(2,1)S(1)}, bf16[256,256]{1,0:T(8,128)(2,1)S(1)}, u32[]{:S(2)}, u32[]{:S(2)}) collective-permute-start(bf16[256,256]{1,0:T(8,128)(2,1)S(1)} %broadcast_select_fusion.12), channel_id=1, source_target_pairs={{24,0},{25,1},{26,2},{27,3},{28,4},{29,5},{30,6},{31,7},{0,8},{1,9... | collective-permute-start | bytes 393224 | tf_op jit(solution)/shard_map/ppermute | solution.py:11
  293.5 10.4 %collective-permute-start.12 = (bf16[256,256]{1,0:T(8,128)(2,1)S(1)}, bf16[256,256]{1,0:T(8,128)(2,1)S(1)}, u32[]{:S(2)}, u32[]{:S(2)}) collective-permute-start(bf16[256,256]{1,0:T(8,128)(2,1)S(1)} %broadcast_select_fusion.5), channel_id=1, source_target_pairs={{30,0},{31,1},{0,2},{1,3},{2,4},{3,5},{4,6},{5,7},{6,8},{7,9},{8,1... | collective-permute-start | bytes 393224 | tf_op jit(solution)/shard_map/ppermute | solution.py:11
  303.9 7.8 %collective-permute-start.13 = (bf16[256,256]{1,0:T(8,128)(2,1)S(1)}, bf16[256,256]{1,0:T(8,128)(2,1)S(1)}, u32[]{:S(2)}, u32[]{:S(2)}) collective-permute-start(bf16[256,256]{1,0:T(8,128)(2,1)S(1)} %broadcast_select_fusion.8), channel_id=1, source_target_pairs={{28,0},{29,1},{30,2},{31,3},{0,4},{1,5},{2,6},{3,7},{4,8},{5,9},{6... | collective-permute-start | bytes 393224 | tf_op jit(solution)/shard_map/ppermute | solution.py:11
  304.8 9.4 %collective-permute-start.15 = (bf16[256,256]{1,0:T(8,128)(2,1)S(1)}, bf16[256,256]{1,0:T(8,128)(2,1)S(1)}, u32[]{:S(2)}, u32[]{:S(2)}) collective-permute-start(bf16[256,256]{1,0:T(8,128)(2,1)S(1)} %bitcast.49), channel_id=1, source_target_pairs={{31,0},{0,1},{1,2},{2,3},{3,4},{4,5},{5,6},{6,7},{7,8},{8,9},{9,10... | collective-permute-start | bytes 393224 | tf_op jit(solution)/shard_map/ppermute | solution.py:11
  311.7 10.6 %collective-permute-start.14 = (bf16[256,256]{1,0:T(8,128)(2,1)S(1)}, bf16[256,256]{1,0:T(8,128)(2,1)S(1)}, u32[]{:S(2)}, u32[]{:S(2)}) collective-permute-start(bf16[256,256]{1,0:T(8,128)(2,1)S(1)} %broadcast_select_fusion.11), channel_id=1, source_target_pairs={{24,0},{25,1},{26,2},{27,3},{28,4},{29,5},{30,6},{31,7},{0,8},{1,9... | collective-permute-start | bytes 393224 | tf_op jit(solution)/shard_map/ppermute | solution.py:11
  314.2 8.0 %collective-permute-start.16 = (bf16[256,256]{1,0:T(8,128)(2,1)S(1)}, bf16[256,256]{1,0:T(8,128)(2,1)S(1)}, u32[]{:S(2)}, u32[]{:S(2)}) collective-permute-start(bf16[256,256]{1,0:T(8,128)(2,1)S(1)} %collective-permute-done.15), channel_id=1, source_target_pairs={{31,0},{0,1},{1,2},{2,3},{3,4},{4,5},{5,6},{6,7},{7,8},{8,9},{9,10... | collective-permute-start | bytes 393224 | tf_op jit(solution)/shard_map/ppermute | solution.py:11
  322.2 8.0 %collective-permute-start.17 = (bf16[256,256]{1,0:T(8,128)(2,1)S(1)}, bf16[256,256]{1,0:T(8,128)(2,1)S(1)}, u32[]{:S(2)}, u32[]{:S(2)}) collective-permute-start(bf16[256,256]{1,0:T(8,128)(2,1)S(1)} %collective-permute-done.16), channel_id=1, source_target_pairs={{31,0},{0,1},{1,2},{2,3},{3,4},{4,5},{5,6},{6,7},{7,8},{8,9},{9,10... | collective-permute-start | bytes 393224 | tf_op jit(solution)/shard_map/ppermute | solution.py:11
  330.2 10.0 %collective-permute-start.18 = (bf16[256,256]{1,0:T(8,128)(2,1)S(1)}, bf16[256,256]{1,0:T(8,128)(2,1)S(1)}, u32[]{:S(2)}, u32[]{:S(2)}) collective-permute-start(bf16[256,256]{1,0:T(8,128)(2,1)S(1)} %broadcast_select_fusion.4), channel_id=1, source_target_pairs={{30,0},{31,1},{0,2},{1,3},{2,4},{3,5},{4,6},{5,7},{6,8},{7,9},{8,1... | collective-permute-start | bytes 393224 | tf_op jit(solution)/shard_map/ppermute | solution.py:11
  340.3 7.7 %collective-permute-start.19 = (bf16[256,256]{1,0:T(8,128)(2,1)S(1)}, bf16[256,256]{1,0:T(8,128)(2,1)S(1)}, u32[]{:S(2)}, u32[]{:S(2)}) collective-permute-start(bf16[256,256]{1,0:T(8,128)(2,1)S(1)} %broadcast_select_fusion.7), channel_id=1, source_target_pairs={{28,0},{29,1},{30,2},{31,3},{0,4},{1,5},{2,6},{3,7},{4,8},{5,9},{6... | collective-permute-start | bytes 393224 | tf_op jit(solution)/shard_map/ppermute | solution.py:11
  348.0 6.8 %collective-permute-start.20 = (bf16[256,256]{1,0:T(8,128)(2,1)S(1)}, bf16[256,256]{1,0:T(8,128)(2,1)S(1)}, u32[]{:S(2)}, u32[]{:S(2)}) collective-permute-start(bf16[256,256]{1,0:T(8,128)(2,1)S(1)} %broadcast_select_fusion.10), channel_id=1, source_target_pairs={{24,0},{25,1},{26,2},{27,3},{28,4},{29,5},{30,6},{31,7},{0,8},{1,9... | collective-permute-start | bytes 393224 | tf_op jit(solution)/shard_map/ppermute | solution.py:11
Sparse Core Ops, SparseCore 0:
  13.8 131.7 all-reduce.1
where the time goes:
time: 363 us
  waiting for transfers between devices  301 us (83%)
  starting transfers between devices  18.4 us (5%)
  other arithmetic  18.1 us (5%)
  between operations  15 us (4%)
  matrix products  9.2 us (3%)
    ppermute x21, waiting for transfers between devices, shifted(): return lax.ppermute(block, axis, route)  166 us
    psum x1, waiting for transfers between devices, shards(): lax.psum(jnp.dot(picker, samples, preferred_element_type=jnp.float32), 'b...  135 us
    ppermute x21, starting transfers between devices, shifted(): return lax.ppermute(block, axis, route)  18.3 us
  transfers between devices with their start and end apart: 22, of which 18 were waited for; matrix products, arithmetic and copies ran while one was open for 2% of the time, Pallas kernels for 0%

commit v1 on v0

--- a/solution.py
+++ b/solution.py
@@ -1,8 +1,16 @@
+import functools
 import math
 import jax
 import jax.numpy as jnp
 from jax import lax
 from jax.sharding import PartitionSpec as P
+
+
+def arrange_the_core(x_part, dev_axis):
+    return lax.all_gather(x_part, dev_axis).sum(axis=0)
+
+
+carry_vectors = functools.partial(arrange_the_core, dev_axis="blk")
 
 
 def shifted(block, axis, distance):
@@ -41,7 +49,7 @@
     picker = jnp.logical_and(
         (owner == mine)[:, None], within[:, None] == jnp.arange(rows, dtype=jnp.int32)[None, :]
     ).astype(jnp.bfloat16)
-    hub_rows = lax.psum(jnp.dot(picker, samples, preferred_element_type=jnp.float32), "blk")
+    hub_rows = carry_vectors(jnp.dot(picker, samples, preferred_element_type=jnp.float32))
     gram = jnp.dot(hub_rows, hub_rows.T, precision=lax.Precision.HIGHEST)
     proj = jnp.dot(samples, hub_rows.astype(jnp.bfloat16).T, preferred_element_type=jnp.float32)
     factor_lower = jnp.linalg.cholesky(gram)

time: 363 us -> 352 us (0.970)
  waiting for transfers between devices: 301 us -> 284 us
  other arithmetic: 18.1 us -> 25.1 us
    psum x1 -> x0, waiting for transfers between devices: 135 us -> none  [shards(): lax.psum(jnp.dot(picker, samples, preferred_element_type=jnp.float32), 'b...]
    all_gather x0 -> x1, waiting for transfers between devices: none -> 118 us  [arrange_the_core(): return lax.all_gather(x_part, dev_axis).sum(axis=0)]
    reduce_sum x0 -> x1, other arithmetic: none -> 6.98 us  [arrange_the_core(): return lax.all_gather(x_part, dev_axis).sum(axis=0)]
where the time goes in v1:
time: 352 us
  waiting for transfers between devices  284 us (81%)
  other arithmetic  25.1 us (7%)
  starting transfers between devices  18.6 us (5%)
  between operations  15 us (4%)
  matrix products  7.95 us (2%)
    ppermute x21, waiting for transfers between devices, shifted(): return lax.ppermute(block, axis, route)  166 us
    all_gather x1, waiting for transfers between devices, arrange_the_core(): return lax.all_gather(x_part, dev_axis).sum(axis=0)  118 us
    ppermute x21, starting transfers between devices, shifted(): return lax.ppermute(block, axis, route)  18.6 us
  transfers between devices with their start and end apart: 22, of which 18 were waited for; matrix products, arithmetic and copies ran while one was open for 2% of the time, Pallas kernels for 0%

profile of v1, /device:TPU:0, one launch (start us, length us, event | category | flops | bytes accessed | tf_op | source)
XLA Modules:
  0.0 351.6 jit_solution(9919794990849196693)
XLA Ops:
  7.2 0.7 and_select_fusion
  7.9 0.7 fusion.50
  8.5 2.4 fusion.40
  10.9 117.6 %all-gather.3.cloned.1.call-done = f32[2048,2048]{1,0:T(8,128)} async-done(((f32[64,2048]{1,0:T(8,128)}), f32[2048,2048]{1,0:T(8,128)}) %all-gather.3.cloned.1.call-update) | async-done | bytes 16777232 | tf_op jit(solution)/shard_map/all_gather | solution.py:10
  128.5 7.0 %reduce_sum.49 = f32[64,2048]{1,0:T(8,128)S(1)} reduce(f32[32,64,2048]{2,1,0:T(8,128)} %bitcast.48, f32[]{:T(128)} %constant.97.clone.1), dimensions={0}, to_apply=%region_0.1 | reduce | flops 4063232 | bytes 17301508 | tf_op jit(solution)/shard_map/reduce_sum | solution.py:10
  135.5 0.6 fusion.51
  136.0 0.4 fusion.37
  136.6 5.8 %cholesky.16 = f32[64,64]{1,0:T(8,128)S(1)} custom-call(f32[64,64]{1,0:T(8,128)S(1)} %fusion.47), custom_call_target="Cholesky" | custom-call | tf_op jit(solution)/shard_map/jit(cholesky)/cholesky | solution.py:55
  142.5 0.6 compare_reduce_fusion
  143.1 0.7 fusion.42
  143.8 4.9 %custom-call.10 = f32[1,64,64]{1,2,0:T(8,128)S(1)} custom-call(f32[1,64,64]{2,1,0:T(8,128)S(1)} %fusion.42), custom_call_target="InvertDiagBlocksLowerTriangular" | custom-call | tf_op jit(solution)/shard_map/jit(_cho_solve)/triangular_solve | solution.py:56
  148.7 0.3 fusion.45
  149.0 0.2 fusion.43
  149.2 2.1 multiply_reduce_fusion.3
  151.2 2.4 collective-permute-start
  154.2 11.7 %collective-permute-done = bf16[256,2048]{1,0:T(8,128)(2,1)S(1)} collective-permute-done((bf16[256,2048]{1,0:T(8,128)(2,1)S(1)}, bf16[256,2048]{1,0:T(8,128)(2,1)S(1)}, u32[]{:S(2)}, u32[]{:S(2)}) %collective-permute-start) | collective-permute-done | bytes 1048608 | tf_op jit(solution)/shard_map/ppermute | solution.py:19
  166.0 1.5 collective-permute-start.1
  167.5 23.9 %collective-permute-done.1 = bf16[256,2048]{1,0:T(8,128)(2,1)S(1)} collective-permute-done((bf16[256,2048]{1,0:T(8,128)(2,1)S(1)}, bf16[256,2048]{1,0:T(8,128)(2,1)S(1)}, u32[]{:S(2)}, u32[]{:S(2)}) %collective-permute-start.1) | collective-permute-done | bytes 1048608 | tf_op jit(solution)/shard_map/ppermute | solution.py:19
  191.6 24.9 %collective-permute-done.2 = bf16[256,2048]{1,0:T(8,128)(2,1)S(1)} collective-permute-done((bf16[256,2048]{1,0:T(8,128)(2,1)S(1)}, bf16[256,2048]{1,0:T(8,128)(2,1)S(1)}, u32[]{:S(2)}, u32[]{:S(2)}) %collective-permute-start.2) | collective-permute-done | bytes 1048608 | tf_op jit(solution)/shard_map/ppermute | solution.py:19
  216.5 1.4 collective-permute-start.3
  218.0 22.6 %collective-permute-done.3 = bf16[256,2048]{1,0:T(8,128)(2,1)S(1)} collective-permute-done((bf16[256,2048]{1,0:T(8,128)(2,1)S(1)}, bf16[256,2048]{1,0:T(8,128)(2,1)S(1)}, u32[]{:S(2)}, u32[]{:S(2)}) %collective-permute-start.3) | collective-permute-done | bytes 1048608 | tf_op jit(solution)/shard_map/ppermute | solution.py:19
  240.6 0.5 multiply_reduce_fusion.2
  241.1 7.1 %collective-permute-start.4 = (bf16[256,2048]{1,0:T(8,128)(2,1)S(1)}, bf16[256,2048]{1,0:T(8,128)(2,1)S(1)}, u32[]{:S(2)}, u32[]{:S(2)}) collective-permute-start(bf16[256,2048]{1,0:T(8,128)(2,1)S(1)} %get-tuple-element.7), channel_id=1, source_target_pairs={{1,0},{2,1},{3,2},{4,3},{5,4},{6,5},{7,6},{8,7},{9,8},{10,9},{11,1... | collective-permute-start | bytes 3145736 | tf_op jit(solution)/shard_map/ppermute | solution.py:19
  248.3 0.5 fusion.6
  248.8 0.5 fusion.5
  249.3 7.6 %collective-permute-done.6 = bf16[256,256]{1,0:T(8,128)(2,1)S(1)} collective-permute-done((bf16[256,256]{1,0:T(8,128)(2,1)S(1)}, bf16[256,256]{1,0:T(8,128)(2,1)S(1)}, u32[]{:S(2)}, u32[]{:S(2)}) %collective-permute-start.6) | collective-permute-done | bytes 131104 | tf_op jit(solution)/shard_map/ppermute | solution.py:19
  257.0 0.9 fusion.11
  257.9 7.6 %collective-permute-done.7 = bf16[256,256]{1,0:T(8,128)(2,1)S(1)} collective-permute-done((bf16[256,256]{1,0:T(8,128)(2,1)S(1)}, bf16[256,256]{1,0:T(8,128)(2,1)S(1)}, u32[]{:S(2)}, u32[]{:S(2)}) %collective-permute-start.7) | collective-permute-done | bytes 131104 | tf_op jit(solution)/shard_map/ppermute | solution.py:19
  265.6 0.3 multiply_reduce_fusion.1
  265.9 0.6 fusion.7
  266.6 5.3 %collective-permute-start.5 = (bf16[256,2048]{1,0:T(8,128)(2,1)S(1)}, bf16[256,2048]{1,0:T(8,128)(2,1)S(1)}, u32[]{:S(2)}, u32[]{:S(2)}) collective-permute-start(bf16[256,2048]{1,0:T(8,128)(2,1)S(1)} %collective-permute-done.4), channel_id=1, source_target_pairs={{1,0},{2,1},{3,2},{4,3},{5,4},{6,5},{7,6},{8,7},{9,8},{10,9},{11,1... | collective-permute-start | bytes 3145736 | tf_op jit(solution)/shard_map/ppermute | solution.py:19
  272.1 2.6 collective-permute-done.10
  274.8 8.0 %collective-permute-done.11 = bf16[256,256]{1,0:T(8,128)(2,1)S(1)} collective-permute-done((bf16[256,256]{1,0:T(8,128)(2,1)S(1)}, bf16[256,256]{1,0:T(8,128)(2,1)S(1)}, u32[]{:S(2)}, u32[]{:S(2)}) %collective-permute-start.11) | collective-permute-done | bytes 131104 | tf_op jit(solution)/shard_map/ppermute | solution.py:19
  282.8 4.6 %collective-permute-done.9 = bf16[256,256]{1,0:T(8,128)(2,1)S(1)} collective-permute-done((bf16[256,256]{1,0:T(8,128)(2,1)S(1)}, bf16[256,256]{1,0:T(8,128)(2,1)S(1)}, u32[]{:S(2)}, u32[]{:S(2)}) %collective-permute-start.9) | collective-permute-done | bytes 131104 | tf_op jit(solution)/shard_map/ppermute | solution.py:19
  287.5 5.4 %collective-permute-done.12 = bf16[256,256]{1,0:T(8,128)(2,1)S(1)} collective-permute-done((bf16[256,256]{1,0:T(8,128)(2,1)S(1)}, bf16[256,256]{1,0:T(8,128)(2,1)S(1)}, u32[]{:S(2)}, u32[]{:S(2)}) %collective-permute-start.12) | collective-permute-done | bytes 131104 | tf_op jit(solution)/shard_map/ppermute | solution.py:19
  293.0 0.3 multiply_reduce_fusion
  293.3 0.6 fusion.8
  293.9 6.9 %collective-permute-done.13 = bf16[256,256]{1,0:T(8,128)(2,1)S(1)} collective-permute-done((bf16[256,256]{1,0:T(8,128)(2,1)S(1)}, bf16[256,256]{1,0:T(8,128)(2,1)S(1)}, u32[]{:S(2)}, u32[]{:S(2)}) %collective-permute-start.13) | collective-permute-done | bytes 131104 | tf_op jit(solution)/shard_map/ppermute | solution.py:19
  300.9 2.2 collective-permute-done.15
  303.3 7.8 %collective-permute-done.16 = bf16[256,256]{1,0:T(8,128)(2,1)S(1)} collective-permute-done((bf16[256,256]{1,0:T(8,128)(2,1)S(1)}, bf16[256,256]{1,0:T(8,128)(2,1)S(1)}, u32[]{:S(2)}, u32[]{:S(2)}) %collective-permute-start.16) | collective-permute-done | bytes 131104 | tf_op jit(solution)/shard_map/ppermute | solution.py:19
  311.1 8.0 %collective-permute-done.17 = bf16[256,256]{1,0:T(8,128)(2,1)S(1)} collective-permute-done((bf16[256,256]{1,0:T(8,128)(2,1)S(1)}, bf16[256,256]{1,0:T(8,128)(2,1)S(1)}, u32[]{:S(2)}, u32[]{:S(2)}) %collective-permute-start.17) | collective-permute-done | bytes 131104 | tf_op jit(solution)/shard_map/ppermute | solution.py:19
  319.1 0.4 fusion.27
  319.5 9.5 %collective-permute-done.18 = bf16[256,256]{1,0:T(8,128)(2,1)S(1)} collective-permute-done((bf16[256,256]{1,0:T(8,128)(2,1)S(1)}, bf16[256,256]{1,0:T(8,128)(2,1)S(1)}, u32[]{:S(2)}, u32[]{:S(2)}) %collective-permute-start.18) | collective-permute-done | bytes 131104 | tf_op jit(solution)/shard_map/ppermute | solution.py:19
  329.1 0.2 fusion.23
  329.3 7.5 %collective-permute-done.19 = bf16[256,256]{1,0:T(8,128)(2,1)S(1)} collective-permute-done((bf16[256,256]{1,0:T(8,128)(2,1)S(1)}, bf16[256,256]{1,0:T(8,128)(2,1)S(1)}, u32[]{:S(2)}, u32[]{:S(2)}) %collective-permute-start.19) | collective-permute-done | bytes 131104 | tf_op jit(solution)/shard_map/ppermute | solution.py:19
  336.9 1.1 copy.14
  338.1 5.5 %collective-permute-done.20 = bf16[256,256]{1,0:T(8,128)(2,1)S(1)} collective-permute-done((bf16[256,256]{1,0:T(8,128)(2,1)S(1)}, bf16[256,256]{1,0:T(8,128)(2,1)S(1)}, u32[]{:S(2)}, u32[]{:S(2)}) %collective-permute-start.20) | collective-permute-done | bytes 131104 | tf_op jit(solution)/shard_map/ppermute | solution.py:19
  343.8 0.9 pad_maximum_fusion.1
  (50 shorter events, 2.1 us)
Async XLA Ops:
  7.2 121.3 %all-gather.3.cloned.1.call-start = ((), (), s32[]{:S(2)}) async-start(), calls=%async_computation | async-start | bytes 17301504 | tf_op jit(solution)/shard_map/all_gather | solution.py:10
  128.5 7.6 %copy-start = (bf16[256,2048]{1,0:T(8,128)(2,1)S(1)}, bf16[256,2048]{1,0:T(8,128)(2,1)}, u32[]{:S(2)}) copy-start(bf16[256,2048]{1,0:T(8,128)(2,1)} %param.3) | copy-start | bytes 3145732
  151.2 14.7 %collective-permute-start = (bf16[256,2048]{1,0:T(8,128)(2,1)S(1)}, bf16[256,2048]{1,0:T(8,128)(2,1)S(1)}, u32[]{:S(2)}, u32[]{:S(2)}) collective-permute-start(bf16[256,2048]{1,0:T(8,128)(2,1)S(1)} %get-tuple-element.9), channel_id=1, source_target_pairs={{1,0},{2,1},{3,2},{4,3},{5,4},{6,5},{7,6},{8,7},{9,8},{10,9},{11,1... | collective-permute-start | bytes 3145736 | tf_op jit(solution)/shard_map/ppermute | solution.py:19
  166.0 25.4 %collective-permute-start.1 = (bf16[256,2048]{1,0:T(8,128)(2,1)S(1)}, bf16[256,2048]{1,0:T(8,128)(2,1)S(1)}, u32[]{:S(2)}, u32[]{:S(2)}) collective-permute-start(bf16[256,2048]{1,0:T(8,128)(2,1)S(1)} %broadcast_select_fusion), channel_id=1, source_target_pairs={{2,0},{3,1},{4,2},{5,3},{6,4},{7,5},{8,6},{9,7},{10,8},{11,9},{12,... | collective-permute-start | bytes 3145736 | tf_op jit(solution)/shard_map/ppermute | solution.py:19
  191.5 24.9 %collective-permute-start.2 = (bf16[256,2048]{1,0:T(8,128)(2,1)S(1)}, bf16[256,2048]{1,0:T(8,128)(2,1)S(1)}, u32[]{:S(2)}, u32[]{:S(2)}) collective-permute-start(bf16[256,2048]{1,0:T(8,128)(2,1)S(1)} %broadcast_select_fusion.1), channel_id=1, source_target_pairs={{4,0},{5,1},{6,2},{7,3},{8,4},{9,5},{10,6},{11,7},{12,8},{13,9},{1... | collective-permute-start | bytes 3145736 | tf_op jit(solution)/shard_map/ppermute | solution.py:19
  216.5 24.1 %collective-permute-start.3 = (bf16[256,2048]{1,0:T(8,128)(2,1)S(1)}, bf16[256,2048]{1,0:T(8,128)(2,1)S(1)}, u32[]{:S(2)}, u32[]{:S(2)}) collective-permute-start(bf16[256,2048]{1,0:T(8,128)(2,1)S(1)} %broadcast_select_fusion.2), channel_id=1, source_target_pairs={{8,0},{9,1},{10,2},{11,3},{12,4},{13,5},{14,6},{15,7},{16,8},{17,9... | collective-permute-start | bytes 3145736 | tf_op jit(solution)/shard_map/ppermute | solution.py:19
  241.1 24.5 %collective-permute-start.4 = (bf16[256,2048]{1,0:T(8,128)(2,1)S(1)}, bf16[256,2048]{1,0:T(8,128)(2,1)S(1)}, u32[]{:S(2)}, u32[]{:S(2)}) collective-permute-start(bf16[256,2048]{1,0:T(8,128)(2,1)S(1)} %get-tuple-element.7), channel_id=1, source_target_pairs={{1,0},{2,1},{3,2},{4,3},{5,4},{6,5},{7,6},{8,7},{9,8},{10,9},{11,1... | collective-permute-start | bytes 3145736 | tf_op jit(solution)/shard_map/ppermute | solution.py:19
  248.8 8.1 %collective-permute-start.6 = (bf16[256,256]{1,0:T(8,128)(2,1)S(1)}, bf16[256,256]{1,0:T(8,128)(2,1)S(1)}, u32[]{:S(2)}, u32[]{:S(2)}) collective-permute-start(bf16[256,256]{1,0:T(8,128)(2,1)S(1)} %bitcast.49), channel_id=1, source_target_pairs={{31,0},{0,1},{1,2},{2,3},{3,4},{4,5},{5,6},{6,7},{7,8},{8,9},{9,10... | collective-permute-start | bytes 393224 | tf_op jit(solution)/shard_map/ppermute | solution.py:19
  256.9 8.6 %collective-permute-start.7 = (bf16[256,256]{1,0:T(8,128)(2,1)S(1)}, bf16[256,256]{1,0:T(8,128)(2,1)S(1)}, u32[]{:S(2)}, u32[]{:S(2)}) collective-permute-start(bf16[256,256]{1,0:T(8,128)(2,1)S(1)} %broadcast_select_fusion.6), channel_id=1, source_target_pairs={{30,0},{31,1},{0,2},{1,3},{2,4},{3,5},{4,6},{5,7},{6,8},{7,9},{8,1... | collective-permute-start | bytes 393224 | tf_op jit(solution)/shard_map/ppermute | solution.py:19
  265.6 9.1 %collective-permute-start.8 = (bf16[256,256]{1,0:T(8,128)(2,1)S(1)}, bf16[256,256]{1,0:T(8,128)(2,1)S(1)}, u32[]{:S(2)}, u32[]{:S(2)}) collective-permute-start(bf16[256,256]{1,0:T(8,128)(2,1)S(1)} %broadcast_select_fusion.9), channel_id=1, source_target_pairs={{28,0},{29,1},{30,2},{31,3},{0,4},{1,5},{2,6},{3,7},{4,8},{5,9},{6... | collective-permute-start | bytes 393224 | tf_op jit(solution)/shard_map/ppermute | solution.py:19
  266.5 8.2 %collective-permute-start.10 = (bf16[256,256]{1,0:T(8,128)(2,1)S(1)}, bf16[256,256]{1,0:T(8,128)(2,1)S(1)}, u32[]{:S(2)}, u32[]{:S(2)}) collective-permute-start(bf16[256,256]{1,0:T(8,128)(2,1)S(1)} %bitcast.50), channel_id=1, source_target_pairs={{31,0},{0,1},{1,2},{2,3},{3,4},{4,5},{5,6},{6,7},{7,8},{8,9},{9,10... | collective-permute-start | bytes 393224 | tf_op jit(solution)/shard_map/ppermute | solution.py:19
  266.6 26.4 %collective-permute-start.5 = (bf16[256,2048]{1,0:T(8,128)(2,1)S(1)}, bf16[256,2048]{1,0:T(8,128)(2,1)S(1)}, u32[]{:S(2)}, u32[]{:S(2)}) collective-permute-start(bf16[256,2048]{1,0:T(8,128)(2,1)S(1)} %collective-permute-done.4), channel_id=1, source_target_pairs={{1,0},{2,1},{3,2},{4,3},{5,4},{6,5},{7,6},{8,7},{9,8},{10,9},{11,1... | collective-permute-start | bytes 3145736 | tf_op jit(solution)/shard_map/ppermute | solution.py:19
  274.7 8.1 %collective-permute-start.11 = (bf16[256,256]{1,0:T(8,128)(2,1)S(1)}, bf16[256,256]{1,0:T(8,128)(2,1)S(1)}, u32[]{:S(2)}, u32[]{:S(2)}) collective-permute-start(bf16[256,256]{1,0:T(8,128)(2,1)S(1)} %collective-permute-done.10), channel_id=1, source_target_pairs={{31,0},{0,1},{1,2},{2,3},{3,4},{4,5},{5,6},{6,7},{7,8},{8,9},{9,10... | collective-permute-start | bytes 393224 | tf_op jit(solution)/shard_map/ppermute | solution.py:19
  274.7 12.8 %collective-permute-start.9 = (bf16[256,256]{1,0:T(8,128)(2,1)S(1)}, bf16[256,256]{1,0:T(8,128)(2,1)S(1)}, u32[]{:S(2)}, u32[]{:S(2)}) collective-permute-start(bf16[256,256]{1,0:T(8,128)(2,1)S(1)} %broadcast_select_fusion.12), channel_id=1, source_target_pairs={{24,0},{25,1},{26,2},{27,3},{28,4},{29,5},{30,6},{31,7},{0,8},{1,9... | collective-permute-start | bytes 393224 | tf_op jit(solution)/shard_map/ppermute | solution.py:19
  282.8 10.1 %collective-permute-start.12 = (bf16[256,256]{1,0:T(8,128)(2,1)S(1)}, bf16[256,256]{1,0:T(8,128)(2,1)S(1)}, u32[]{:S(2)}, u32[]{:S(2)}) collective-permute-start(bf16[256,256]{1,0:T(8,128)(2,1)S(1)} %broadcast_select_fusion.5), channel_id=1, source_target_pairs={{30,0},{31,1},{0,2},{1,3},{2,4},{3,5},{4,6},{5,7},{6,8},{7,9},{8,1... | collective-permute-start | bytes 393224 | tf_op jit(solution)/shard_map/ppermute | solution.py:19
  292.9 7.9 %collective-permute-start.13 = (bf16[256,256]{1,0:T(8,128)(2,1)S(1)}, bf16[256,256]{1,0:T(8,128)(2,1)S(1)}, u32[]{:S(2)}, u32[]{:S(2)}) collective-permute-start(bf16[256,256]{1,0:T(8,128)(2,1)S(1)} %broadcast_select_fusion.8), channel_id=1, source_target_pairs={{28,0},{29,1},{30,2},{31,3},{0,4},{1,5},{2,6},{3,7},{4,8},{5,9},{6... | collective-permute-start | bytes 393224 | tf_op jit(solution)/shard_map/ppermute | solution.py:19
  293.9 9.2 %collective-permute-start.15 = (bf16[256,256]{1,0:T(8,128)(2,1)S(1)}, bf16[256,256]{1,0:T(8,128)(2,1)S(1)}, u32[]{:S(2)}, u32[]{:S(2)}) collective-permute-start(bf16[256,256]{1,0:T(8,128)(2,1)S(1)} %bitcast.51), channel_id=1, source_target_pairs={{31,0},{0,1},{1,2},{2,3},{3,4},{4,5},{5,6},{6,7},{7,8},{8,9},{9,10... | collective-permute-start | bytes 393224 | tf_op jit(solution)/shard_map/ppermute | solution.py:19
  300.8 10.3 %collective-permute-start.14 = (bf16[256,256]{1,0:T(8,128)(2,1)S(1)}, bf16[256,256]{1,0:T(8,128)(2,1)S(1)}, u32[]{:S(2)}, u32[]{:S(2)}) collective-permute-start(bf16[256,256]{1,0:T(8,128)(2,1)S(1)} %broadcast_select_fusion.11), channel_id=1, source_target_pairs={{24,0},{25,1},{26,2},{27,3},{28,4},{29,5},{30,6},{31,7},{0,8},{1,9... | collective-permute-start | bytes 393224 | tf_op jit(solution)/shard_map/ppermute | solution.py:19
  303.1 8.0 %collective-permute-start.16 = (bf16[256,256]{1,0:T(8,128)(2,1)S(1)}, bf16[256,256]{1,0:T(8,128)(2,1)S(1)}, u32[]{:S(2)}, u32[]{:S(2)}) collective-permute-start(bf16[256,256]{1,0:T(8,128)(2,1)S(1)} %collective-permute-done.15), channel_id=1, source_target_pairs={{31,0},{0,1},{1,2},{2,3},{3,4},{4,5},{5,6},{6,7},{7,8},{8,9},{9,10... | collective-permute-start | bytes 393224 | tf_op jit(solution)/shard_map/ppermute | solution.py:19
  311.1 8.0 %collective-permute-start.17 = (bf16[256,256]{1,0:T(8,128)(2,1)S(1)}, bf16[256,256]{1,0:T(8,128)(2,1)S(1)}, u32[]{:S(2)}, u32[]{:S(2)}) collective-permute-start(bf16[256,256]{1,0:T(8,128)(2,1)S(1)} %collective-permute-done.16), channel_id=1, source_target_pairs={{31,0},{0,1},{1,2},{2,3},{3,4},{4,5},{5,6},{6,7},{7,8},{8,9},{9,10... | collective-permute-start | bytes 393224 | tf_op jit(solution)/shard_map/ppermute | solution.py:19
  319.1 10.0 %collective-permute-start.18 = (bf16[256,256]{1,0:T(8,128)(2,1)S(1)}, bf16[256,256]{1,0:T(8,128)(2,1)S(1)}, u32[]{:S(2)}, u32[]{:S(2)}) collective-permute-start(bf16[256,256]{1,0:T(8,128)(2,1)S(1)} %broadcast_select_fusion.4), channel_id=1, source_target_pairs={{30,0},{31,1},{0,2},{1,3},{2,4},{3,5},{4,6},{5,7},{6,8},{7,9},{8,1... | collective-permute-start | bytes 393224 | tf_op jit(solution)/shard_map/ppermute | solution.py:19
  329.1 7.7 %collective-permute-start.19 = (bf16[256,256]{1,0:T(8,128)(2,1)S(1)}, bf16[256,256]{1,0:T(8,128)(2,1)S(1)}, u32[]{:S(2)}, u32[]{:S(2)}) collective-permute-start(bf16[256,256]{1,0:T(8,128)(2,1)S(1)} %broadcast_select_fusion.7), channel_id=1, source_target_pairs={{28,0},{29,1},{30,2},{31,3},{0,4},{1,5},{2,6},{3,7},{4,8},{5,9},{6... | collective-permute-start | bytes 393224 | tf_op jit(solution)/shard_map/ppermute | solution.py:19
  336.8 6.8 %collective-permute-start.20 = (bf16[256,256]{1,0:T(8,128)(2,1)S(1)}, bf16[256,256]{1,0:T(8,128)(2,1)S(1)}, u32[]{:S(2)}, u32[]{:S(2)}) collective-permute-start(bf16[256,256]{1,0:T(8,128)(2,1)S(1)} %broadcast_select_fusion.10), channel_id=1, source_target_pairs={{24,0},{25,1},{26,2},{27,3},{28,4},{29,5},{30,6},{31,7},{0,8},{1,9... | collective-permute-start | bytes 393224 | tf_op jit(solution)/shard_map/ppermute | solution.py:19
Sparse Core Ops, SparseCore 0:
  11.4 117.0 all-gather.2
